TPU v7x, 32 devices: a whole 2x2x4 slice. The times are simulated.
32 devices in a mesh: ao: 8 (over y, x, core), aux: 4 (over z).
Axes of the slice: x: 2, y: 2, z: 4, core: 2. Of those that a mesh axis runs over, the one named last changes fastest.
Arguments:
- blocks: bfloat16 [48, 256, 128, 128], P('ao', 'aux'), may hold values from -6 to 6
- pairs: int32 [48, 2], P('ao'), may hold values from 0 to 79, as said below
- counts: int32 [8], P('ao'), may hold values from 1 to 6, as said below
- owned_blocks: int32 [80], P('ao'), may hold values from 0 to 79, as said below
- occ_coef: bfloat16 [80, 8, 128], P('ao'), may hold values from -0.5 to 0.5
- vir_coef: bfloat16 [10240, 9216], P('ao', 'aux'), may hold values from -0.109375 to 0.109375
Outputs:
- b_tensor: bfloat16 [256, 8, 9216], P('ao', None, 'aux')
Inputs may be any that keep to these rules, and one draw needn't show every extreme that they name: `pairs`: among the used slots of one ao index, at most 3 have nu blocks whose rows one owner holds; in every draw some index reaches 3. `counts`: some ao index uses all 6 slots in every draw. `owned_blocks`: every atom block appears exactly once.
All inputs are finite; a program needn't handle non-finite values.
Results may differ from a plain program's by a relative error of at most 0.014.
Values may be sent and summed in bfloat16 or wider, within the bound.
A program may use at most 128 MiB of HBM per device.

v0:
```python
import jax
import jax.numpy as jnp
from jax import lax
from jax.sharding import PartitionSpec as P


def block_place(block_ids, owned_all):
    hits = block_ids[..., None] == owned_all
    positions = jnp.arange(owned_all.shape[0], dtype=jnp.int32)
    return jnp.sum(jnp.where(hits, positions, 0), axis=-1)


def per_device(blocks, pairs, counts, owned_blocks, occ_coef, vir_coef):
    groups = lax.axis_size("ao")
    own_index = lax.axis_index("ao")
    slot_count = blocks.shape[0]
    aux_depth = blocks.shape[1]
    block_width = blocks.shape[3]
    occupied = occ_coef.shape[1]
    all_pairs, all_counts, all_owned = (
        lax.all_gather(pairs, "ao", axis=0, tiled=True),
        lax.all_gather(counts, "ao", axis=0, tiled=True),
        lax.all_gather(owned_blocks, "ao", axis=0, tiled=True),
    )
    occ_all = lax.all_gather(occ_coef, "ao", axis=0, tiled=True)
    total_blocks = all_owned.shape[0]
    per_owner = total_blocks // groups
    slot_ids = jnp.arange(slot_count, dtype=jnp.int32)
    in_use = slot_ids < counts[0]
    occ_pick = occ_all[block_place(pairs[:, 0], all_owned)]
    slab_values = jnp.einsum("sim,spmn->spin", occ_pick, blocks, preferred_element_type=jnp.float32)
    slab_values = jnp.where(in_use[:, None, None, None], slab_values, 0.0).astype(jnp.bfloat16)
    flat_slabs = slab_values.reshape(slot_count, aux_depth * occupied, block_width)
    place_all = block_place(all_pairs[:, 1], all_owned).reshape(groups, slot_count)
    owner_all = place_all // per_owner
    local_all = place_all % per_owner
    live_all = slot_ids[None, :] < all_counts[:, None]
    mine_all = live_all & (owner_all == own_index)
    local_ids = jnp.arange(per_owner, dtype=jnp.int32)
    slabs_got = lax.all_gather(flat_slabs, "ao", axis=0, tiled=True)
    assign = (
        mine_all.reshape(-1)[None, :] & (local_all.reshape(-1)[None, :] == local_ids[:, None])
    ).astype(jnp.bfloat16)
    summed = jnp.einsum("lt,tqm->qlm", assign, slabs_got, preferred_element_type=jnp.float32)
    rows_local = summed.reshape(summed.shape[0], per_owner * block_width).astype(jnp.bfloat16)
    rows_whole = lax.all_gather(rows_local, "aux", axis=0, tiled=True)
    share = rows_whole.shape[0] // groups
    result = lax.psum_scatter(
        jnp.dot(rows_whole, vir_coef, preferred_element_type=jnp.float32).astype(jnp.bfloat16),
        "ao",
        scatter_dimension=0,
        tiled=True,
    ).astype(jnp.float32)
    return result.reshape(share // occupied, occupied, vir_coef.shape[1]).astype(jnp.bfloat16)


def solution(mesh):
    in_specs = (
        P("ao", "aux", None, None),
        P("ao", None),
        P("ao"),
        P("ao"),
        P("ao", None, None),
        P("ao", "aux"),
    )
    out_specs = P("ao", None, "aux")
    return jax.shard_map(
        per_device, mesh=mesh, in_specs=in_specs, out_specs=out_specs, check_vma=False
    )
```

profile of v0, /device:TPU:0, one launch (start us, length us, event | category | flops | bytes accessed | tf_op | source)
XLA Modules:
  0.0 291.0 jit_solution(9892513670469097050)
XLA Ops:
  6.5 0.0 all-gather.4.cloned.1.call-start
  7.2 0.7 slice_bitcast_fusion.1
  7.9 1.3 dynamic-slice
  9.9 0.8 dynamic-update-slice.1
  10.7 0.8 dynamic-update-slice
  11.5 9.5 %all-reduce.2 = (s32[80]{0:T(128)S(1)}, s32[8]{0:T(128)S(1)}) all-reduce(s32[80]{0:T(128)S(1)} %dynamic-update-slice, s32[8]{0:T(128)S(1)} %dynamic-update-slice.1), channel_id=1, replica_groups=mesh['ao'=8,'aux'=4] {'ao'}, use_global_device_ids=true, to_apply=%add | all-reduce | flops 88 | bytes 704
  21.0 0.2 select_reduce_fusion.1
  21.2 8.6 %all_gather.18 = bf16[80,8,128]{2,1,0:T(8,128)(2,1)S(1)} all-gather(bf16[10,8,128]{2,1,0:T(8,128)(2,1)} %param.10), channel_id=1, replica_groups=mesh['ao'=8,'aux'=4] {'ao'}, dimensions={0}, use_global_device_ids=true | all-gather | bytes 184320 | tf_op jit(solution)/shard_map/all_gather | solution.py:25
  29.8 0.6 gather_fusion
  30.4 0.0 copy-start
  30.4 7.2 %fusion.4 = bf16[6,512,128]{2,1,0:T(8,128)(2,1)} fusion(bf16[6,64,128,128]{3,2,1,0:T(8,128)(2,1)} %param.6, pred[6]{0:T(512)(128)(4,1)S(1)} %iota_compare_fusion.2, bf16[6,8,128]{2,1,0:T(8,128)(2,1)S(1)} %gather_fusion), kind=kOutput, calls=%fused_computation.6 | convolution fusion | flops 101449728 | bytes 13381638 | tf_op jit(solution)/shard_map/sim,spmn->spin/dot_general | solution.py:31
  37.6 0.0 all-gather.4.cloned.1.call-update
  37.6 0.0 all-gather.6.cloned.1.call-start
  37.7 0.1 iota_compare_fusion.1
  37.8 0.1 lt.52
  37.9 0.0 copy-done
  37.9 8.6 %all-gather = s32[8,6,2]{1,2,0:T(2,128)S(1)} all-gather(s32[1,6,2]{1,2,0:T(2,128)S(1)} %bitcast.35), channel_id=1, replica_groups=mesh['ao'=8,'aux'=4] {'ao'}, dimensions={0}, use_global_device_ids=true | all-gather | bytes 432 | tf_op jit(solution)/shard_map/all_gather | solution.py:21
  46.5 0.1 reshape.75
  46.5 0.2 select_reduce_fusion
  46.8 36.7 %all-gather.4.cloned.1.call-done = bf16[48,512,128]{2,1,0:T(8,128)(2,1)} async-done(((bf16[6,512,128]{2,1,0:T(8,128)(2,1)}), bf16[48,512,128]{2,1,0:T(8,128)(2,1)}) %all-gather.4.cloned.1.call-update) | async-done | bytes 6291472 | tf_op jit(solution)/shard_map/all_gather | solution.py:40
  83.5 6.4 %convert_bitcast_fusion = bf16[512,10,128]{2,1,0:T(8,128)(2,1)S(1)} fusion(bf16[48,512,128]{2,1,0:T(8,128)(2,1)} %all-gather.4.cloned.1.call-done, s32[48]{0:T(128)S(1)} %and_select_fusion, pred[48]{0:T(512)(128)(4,1)S(1)} %compare_and_fusion), kind=kOutput, calls=%fused_computation.4 | convolution fusion | flops 63570880 | bytes 7602416 | tf_op jit(solution)/shard_map/lt,tqm->qlm/dot_general | solution.py:44
  89.9 2.6 copy.17
  92.5 0.0 all-gather.6.cloned.1.call-update
  92.5 0.2 reduce-scatter.2.cloned.1.call-start
  92.7 98.0 %all-gather.6.cloned.1.call-done = bf16[2048,1280]{0,1:T(8,128)(2,1)} async-done(((bf16[512,1280]{0,1:T(8,128)(2,1)}), bf16[2048,1280]{0,1:T(8,128)(2,1)}) %all-gather.6.cloned.1.call-update) | async-done | bytes 5242896 | tf_op jit(solution)/shard_map/all_gather | solution.py:46
  190.7 18.4 %convolution_convert_fusion = bf16[2048,2304]{1,0:T(8,128)(2,1)} fusion(bf16[2048,1280]{0,1:T(8,128)(2,1)} %all-gather.6.cloned.1.call-done, bf16[1280,2304]{1,0:T(8,128)(2,1)} %param.11), kind=kOutput, calls=%fused_computation.1 | convolution fusion | flops 12084314112 | bytes 20578304 | tf_op jit(solution)/shard_map/dot_general | solution.py:49
  209.1 0.0 reduce-scatter.2.cloned.1.call-update
  209.1 75.3 %reduce-scatter.2.cloned.1.call-done = bf16[256,2304]{1,0:T(8,128)(2,1)} async-done(((bf16[2048,2304]{1,0:T(8,128)(2,1)}), bf16[256,2304]{1,0:T(8,128)(2,1)}) %reduce-scatter.2.cloned.1.call-update) | async-done | bytes 1179664 | tf_op jit(solution)/shard_map/reduce_scatter | solution.py:48
  (9 shorter events, 0.1 us)
Async XLA Ops:
  6.5 76.9 %all-gather.4.cloned.1.call-start = ((), (), s32[]{:S(2)}) async-start(), calls=%async_computation.1 | async-start | bytes 7077888 | tf_op jit(solution)/shard_map/all_gather | solution.py:40
  30.4 7.5 %copy-start = (s32[6,2]{0,1:T(2,128)S(1)}, s32[6,2]{0,1:T(2,128)}, u32[]{:S(2)}) copy-start(s32[6,2]{0,1:T(2,128)} %param.7) | copy-start | bytes 148
  37.6 153.0 %all-gather.6.cloned.1.call-start = ((), (), s32[]{:S(2)}) async-start(), calls=%async_computation.2 | async-start | bytes 6553600 | tf_op jit(solution)/shard_map/all_gather | solution.py:46
  92.5 191.9 %reduce-scatter.2.cloned.1.call-start = ((), (), s32[]{:S(2)}) async-start(), calls=%async_computation.3 | async-start | bytes 10616832 | tf_op jit(solution)/shard_map/reduce_scatter | solution.py:48
Sparse Core Ops, SparseCore 0:
  37.8 45.6 all-gather.3
  92.6 98.0 all-gather.5
  209.2 75.1 reduce-scatter.1
where the time goes:
time: 291 us
  waiting for transfers between devices  210 us (72%)
  matrix products  32.1 us (11%)
  blocking collectives  26.7 us (9%)
  between operations  14.5 us (5%)
  local copies, waits for them, and re-layouts  6.95 us (2%)
    all_gather x1, waiting for transfers between devices, per_device(): rows_whole = lax.all_gather(rows_local, 'aux', axis=0, tiled=True)  98 us
    reduce_scatter x1, waiting for transfers between devices, per_device(): lax.psum_scatter(jnp.dot(rows_whole, vir_coef, preferred_element_type=jnp...  75.3 us
    all_gather x1, waiting for transfers between devices, per_device(): slabs_got = lax.all_gather(flat_slabs, 'ao', axis=0, tiled=True)  36.7 us
    dot_general x1, matrix products, per_device(): jnp.dot(rows_whole, vir_coef, preferred_element_type=jnp.float32)  18.4 us
    unnamed x1, blocking collectives  9.49 us
    all_gather x1, blocking collectives, per_device(): occ_all = lax.all_gather(occ_coef, 'ao', axis=0, tiled=True)  8.6 us
    all_gather x1, blocking collectives, per_device(): lax.all_gather(pairs, 'ao', axis=0, tiled=True)  8.59 us
    dot_general x1, matrix products, per_device(): jnp.einsum('sim,spmn->spin', occ_pick, blocks, preferred_element_type=jnp...  7.2 us
  transfers between devices with their start and end apart: 3, of which 3 were waited for; matrix products, arithmetic and copies ran while one was open for 0% of the time, Pallas kernels for 0%

commit v1 on v0

--- a/solution.py
+++ b/solution.py
@@ -43,7 +43,16 @@
     ).astype(jnp.bfloat16)
     summed = jnp.einsum("lt,tqm->qlm", assign, slabs_got, preferred_element_type=jnp.float32)
     rows_local = summed.reshape(summed.shape[0], per_owner * block_width).astype(jnp.bfloat16)
-    rows_whole = lax.all_gather(rows_local, "aux", axis=0, tiled=True)
+    nodes = jax.lax.axis_size("aux")
+    table = [rows_local]
+    d = 1
+    while d < nodes:
+        table.append(
+            jax.lax.ppermute(table[d - 1], "aux", [(no, (no - 1) % nodes) for no in range(nodes)])
+        )
+        d = d + 1
+    all_values = jnp.concatenate(table, axis=0)
+    rows_whole = jnp.roll(all_values, jax.lax.axis_index("aux") * rows_local.shape[0], axis=0)
     share = rows_whole.shape[0] // groups
     result = lax.psum_scatter(
         jnp.dot(rows_whole, vir_coef, preferred_element_type=jnp.float32).astype(jnp.bfloat16),

time: 291 us -> 292 us (level)
  waiting for transfers between devices: 210 us -> 196 us
  starting transfers between devices: 0.27 us -> 12.1 us
  local copies, waits for them, and re-layouts: 6.95 us -> 12.6 us
  matrix products: 32.1 us -> 28.9 us
    all_gather x1 -> x0, waiting for transfers between devices: 98 us -> none  [per_device(): rows_whole = lax.all_gather(rows_local, 'aux', axis=0, tiled=True)]
    ppermute x0 -> x3, waiting for transfers between devices: none -> 81.1 us  [per_device(): jax.lax.ppermute(table[d - 1], 'aux', [(no, (no - 1) % nodes) for no in r...]
    ppermute x0 -> x3, starting transfers between devices: none -> 12 us  [per_device(): jax.lax.ppermute(table[d - 1], 'aux', [(no, (no - 1) % nodes) for no in r...]
    unnamed x8 -> x19, local copies, waits for them, and re-layouts: 3.05 us -> 8.28 us
    dot_general x1, matrix products: 18.4 us -> 15.2 us  [per_device(): jnp.dot(rows_whole, vir_coef, preferred_element_type=jnp.float32)]
  transfers between devices with their start and end apart: 3 -> 5, of which waited for: 3 -> 5; matrix products, arithmetic and copies ran while one was open for 0% -> 1% of each run, Pallas kernels for 0% -> 0%
where the time goes in v1:
time: 292 us; the launch traced here: 291 us
  waiting for transfers between devices  196 us (67%)
  matrix products  28.9 us (10%)
  blocking collectives  26.7 us (9%)
  between operations  14.8 us (5%)
  local copies, waits for them, and re-layouts  12.6 us (4%)
  starting transfers between devices  12.1 us (4%)
    ppermute x3, waiting for transfers between devices, per_device(): jax.lax.ppermute(table[d - 1], 'aux', [(no, (no - 1) % nodes) for no in r...  81.1 us
    reduce_scatter x1, waiting for transfers between devices, per_device(): lax.psum_scatter(jnp.dot(rows_whole, vir_coef, preferred_element_type=jnp...  77.9 us
    all_gather x1, waiting for transfers between devices, per_device(): slabs_got = lax.all_gather(flat_slabs, 'ao', axis=0, tiled=True)  36.7 us
    dot_general x1, matrix products, per_device(): jnp.dot(rows_whole, vir_coef, preferred_element_type=jnp.float32)  15.2 us
    ppermute x3, starting transfers between devices, per_device(): jax.lax.ppermute(table[d - 1], 'aux', [(no, (no - 1) % nodes) for no in r...  12 us
    unnamed x1, blocking collectives  9.49 us
    all_gather x1, blocking collectives, per_device(): occ_all = lax.all_gather(occ_coef, 'ao', axis=0, tiled=True)  8.6 us
    all_gather x1, blocking collectives, per_device(): lax.all_gather(pairs, 'ao', axis=0, tiled=True)  8.59 us
  transfers between devices with their start and end apart: 5, of which 5 were waited for; matrix products, arithmetic and copies ran while one was open for 1% of the time, Pallas kernels for 0%

profile of v1, /device:TPU:0, one launch (start us, length us, event | category | flops | bytes accessed | tf_op | source)
XLA Modules:
  0.0 291.3 jit_solution(16555827852540722931)
XLA Ops:
  7.2 0.7 slice_bitcast_fusion.1
  7.9 1.3 dynamic-slice
  9.8 0.7 dynamic-update-slice.1
  10.5 0.8 dynamic-update-slice
  11.3 9.5 %all-reduce.2 = (s32[80]{0:T(128)S(1)}, s32[8]{0:T(128)S(1)}) all-reduce(s32[80]{0:T(128)S(1)} %dynamic-update-slice, s32[8]{0:T(128)S(1)} %dynamic-update-slice.1), channel_id=1, replica_groups=mesh['ao'=8,'aux'=4] {'ao'}, use_global_device_ids=true, to_apply=%add | all-reduce | flops 88 | bytes 704
  20.8 0.2 select_reduce_fusion.1
  21.0 8.6 %all_gather.15 = bf16[80,8,128]{2,1,0:T(8,128)(2,1)S(1)} all-gather(bf16[10,8,128]{2,1,0:T(8,128)(2,1)} %param.10), channel_id=1, replica_groups=mesh['ao'=8,'aux'=4] {'ao'}, dimensions={0}, use_global_device_ids=true | all-gather | bytes 184320 | tf_op jit(solution)/shard_map/all_gather | solution.py:25
  29.6 0.6 gather_fusion
  30.2 7.2 %fusion.5 = bf16[6,512,128]{2,1,0:T(8,128)(2,1)} fusion(bf16[6,64,128,128]{3,2,1,0:T(8,128)(2,1)} %param.6, pred[6]{0:T(512)(128)(4,1)S(1)} %iota_compare_fusion.2, bf16[6,8,128]{2,1,0:T(8,128)(2,1)S(1)} %gather_fusion), kind=kOutput, calls=%fused_computation.7 | convolution fusion | flops 101449728 | bytes 13381638 | tf_op jit(solution)/shard_map/sim,spmn->spin/dot_general | solution.py:31
  37.5 0.1 lt.64
  37.6 8.6 %all-gather = s32[8,6,2]{1,2,0:T(2,128)S(1)} all-gather(s32[1,6,2]{1,2,0:T(2,128)S(1)} %bitcast.36), channel_id=1, replica_groups=mesh['ao'=8,'aux'=4] {'ao'}, dimensions={0}, use_global_device_ids=true | all-gather | bytes 432 | tf_op jit(solution)/shard_map/all_gather | solution.py:21
  46.2 0.1 reshape.75
  46.3 0.2 select_reduce_fusion
  46.5 36.7 %all-gather.3.cloned.1.call-done = bf16[48,512,128]{2,1,0:T(8,128)(2,1)} async-done(((bf16[6,512,128]{2,1,0:T(8,128)(2,1)}), bf16[48,512,128]{2,1,0:T(8,128)(2,1)}) %all-gather.3.cloned.1.call-update) | async-done | bytes 6291472 | tf_op jit(solution)/shard_map/all_gather | solution.py:40
  83.2 6.4 %convert_bitcast_fusion = bf16[512,10,128]{2,1,0:T(8,128)(2,1)S(1)} fusion(bf16[48,512,128]{2,1,0:T(8,128)(2,1)} %all-gather.3.cloned.1.call-done, s32[48]{0:T(128)S(1)} %and_select_fusion, pred[48]{0:T(512)(128)(4,1)S(1)} %compare_and_fusion), kind=kOutput, calls=%fused_computation.5 | convolution fusion | flops 63570880 | bytes 7602416 | tf_op jit(solution)/shard_map/lt,tqm->qlm/dot_general | solution.py:44
  89.7 1.5 copy.17
  91.2 3.4 %collective-permute-start = (bf16[512,1280]{0,1:T(8,128)(2,1)S(1)}, bf16[512,1280]{0,1:T(8,128)(2,1)S(1)}, u32[]{:S(2)}, u32[]{:S(2)}) collective-permute-start(bf16[512,1280]{0,1:T(8,128)(2,1)S(1)} %bitcast.33), channel_id=1, source_target_pairs={{0,3},{1,0},{2,1},{3,2},{4,7},{5,4},{6,5},{7,6},{8,11},{9,8},{10,9... | collective-permute-start | bytes 3932168 | tf_op jit(solution)/shard_map/ppermute | solution.py:51
  94.6 28.5 %collective-permute-done = bf16[512,1280]{0,1:T(8,128)(2,1)S(1)} collective-permute-done((bf16[512,1280]{0,1:T(8,128)(2,1)S(1)}, bf16[512,1280]{0,1:T(8,128)(2,1)S(1)}, u32[]{:S(2)}, u32[]{:S(2)}) %collective-permute-start) | collective-permute-done | bytes 1310752 | tf_op jit(solution)/shard_map/ppermute | solution.py:51
  123.0 4.3 %collective-permute-start.1 = (bf16[512,1280]{0,1:T(8,128)(2,1)S(1)}, bf16[512,1280]{0,1:T(8,128)(2,1)}, u32[]{:S(2)}, u32[]{:S(2)}) collective-permute-start(bf16[512,1280]{0,1:T(8,128)(2,1)S(1)} %collective-permute-done), channel_id=1, source_target_pairs={{0,3},{1,0},{2,1},{3,2},{4,7},{5,4},{6,5},{7,6},{8,11},{9,8},{10,9... | collective-permute-start | bytes 3932168 | tf_op jit(solution)/shard_map/ppermute | solution.py:51
  127.3 27.6 %collective-permute-done.1 = bf16[512,1280]{0,1:T(8,128)(2,1)} collective-permute-done((bf16[512,1280]{0,1:T(8,128)(2,1)S(1)}, bf16[512,1280]{0,1:T(8,128)(2,1)}, u32[]{:S(2)}, u32[]{:S(2)}) %collective-permute-start.1) | collective-permute-done | bytes 1310752 | tf_op jit(solution)/shard_map/ppermute | solution.py:51
  154.9 4.4 %collective-permute-start.2 = (bf16[512,1280]{0,1:T(8,128)(2,1)}, bf16[512,1280]{0,1:T(8,128)(2,1)}, u32[]{:S(2)}, u32[]{:S(2)}) collective-permute-start(bf16[512,1280]{0,1:T(8,128)(2,1)} %collective-permute-done.1), channel_id=1, source_target_pairs={{0,3},{1,0},{2,1},{3,2},{4,7},{5,4},{6,5},{7,6},{8,11},{9,8},{10,9... | collective-permute-start | bytes 3932168 | tf_op jit(solution)/shard_map/ppermute | solution.py:51
  159.3 0.2 constant_dynamic-update-slice_fusion.7
  159.5 0.2 constant_dynamic-update-slice_fusion.6
  159.6 1.6 constant_dynamic-update-slice_fusion.5
  161.3 25.1 %collective-permute-done.2 = bf16[512,1280]{0,1:T(8,128)(2,1)} collective-permute-done((bf16[512,1280]{0,1:T(8,128)(2,1)}, bf16[512,1280]{0,1:T(8,128)(2,1)}, u32[]{:S(2)}, u32[]{:S(2)}) %collective-permute-start.2) | collective-permute-done | bytes 1310752 | tf_op jit(solution)/shard_map/ppermute | solution.py:51
  186.3 1.5 constant_dynamic-update-slice_fusion.4
  187.8 0.2 constant_dynamic-update-slice_fusion.3
  188.0 0.2 constant_dynamic-update-slice_fusion.2
  188.2 1.6 constant_dynamic-update-slice_fusion.1
  189.8 1.5 constant_dynamic-update-slice_fusion
  191.3 15.2 %convolution_convert_fusion = bf16[2048,2304]{1,0:T(8,128)(2,1)} fusion(bf16[1280,2304]{1,0:T(8,128)(2,1)S(1)} %bitcast.38, bf16[4096,1280]{0,1:T(8,128)(2,1)S(1)} %constant_dynamic-update-slice_fusion, s32[]{:T(128)S(6)} %select_n.62), kind=kOutput, calls=%fused_computation.1 | convolution fusion | flops 12084314112 | bytes 20578308 | tf_op jit(solution)/shard_map/dot_general | solution.py:58
  206.6 77.9 %reduce-scatter.2.cloned.1.call-done = bf16[256,2304]{1,0:T(8,128)(2,1)} async-done(((bf16[2048,2304]{1,0:T(8,128)(2,1)}), bf16[256,2304]{1,0:T(8,128)(2,1)}) %reduce-scatter.2.cloned.1.call-update) | async-done | bytes 1179664 | tf_op jit(solution)/shard_map/reduce_scatter | solution.py:57
  (21 shorter events, 0.2 us)
Async XLA Ops:
  6.5 31.1 %copy-start = (s32[6,2]{0,1:T(2,128)S(1)}, s32[6,2]{0,1:T(2,128)}, u32[]{:S(2)}) copy-start(s32[6,2]{0,1:T(2,128)} %param.7) | copy-start | bytes 148
  6.5 76.7 %all-gather.3.cloned.1.call-start = ((), (), s32[]{:S(2)}) async-start(), calls=%async_computation.1 | async-start | bytes 7077888 | tf_op jit(solution)/shard_map/all_gather | solution.py:40
  37.4 247.1 %reduce-scatter.2.cloned.1.call-start = ((), (), s32[]{:S(2)}) async-start(), calls=%async_computation.2 | async-start | bytes 10616832 | tf_op jit(solution)/shard_map/reduce_scatter | solution.py:57
  91.2 31.8 %collective-permute-start = (bf16[512,1280]{0,1:T(8,128)(2,1)S(1)}, bf16[512,1280]{0,1:T(8,128)(2,1)S(1)}, u32[]{:S(2)}, u32[]{:S(2)}) collective-permute-start(bf16[512,1280]{0,1:T(8,128)(2,1)S(1)} %bitcast.33), channel_id=1, source_target_pairs={{0,3},{1,0},{2,1},{3,2},{4,7},{5,4},{6,5},{7,6},{8,11},{9,8},{10,9... | collective-permute-start | bytes 3932168 | tf_op jit(solution)/shard_map/ppermute | solution.py:51
  123.0 31.9 %collective-permute-start.1 = (bf16[512,1280]{0,1:T(8,128)(2,1)S(1)}, bf16[512,1280]{0,1:T(8,128)(2,1)}, u32[]{:S(2)}, u32[]{:S(2)}) collective-permute-start(bf16[512,1280]{0,1:T(8,128)(2,1)S(1)} %collective-permute-done), channel_id=1, source_target_pairs={{0,3},{1,0},{2,1},{3,2},{4,7},{5,4},{6,5},{7,6},{8,11},{9,8},{10,9... | collective-permute-start | bytes 3932168 | tf_op jit(solution)/shard_map/ppermute | solution.py:51
  154.9 31.4 %collective-permute-start.2 = (bf16[512,1280]{0,1:T(8,128)(2,1)}, bf16[512,1280]{0,1:T(8,128)(2,1)}, u32[]{:S(2)}, u32[]{:S(2)}) collective-permute-start(bf16[512,1280]{0,1:T(8,128)(2,1)} %collective-permute-done.1), channel_id=1, source_target_pairs={{0,3},{1,0},{2,1},{3,2},{4,7},{5,4},{6,5},{7,6},{8,11},{9,8},{10,9... | collective-permute-start | bytes 3932168 | tf_op jit(solution)/shard_map/ppermute | solution.py:51
  159.4 31.8 %slice-start = ((s8[5898240]{0:T(1024)(128)(4,1)}), s8[4194304]{0:T(1024)(128)(4,1)S(1)}, s32[]{:S(2)}) async-start(s8[5898240]{0:T(1024)(128)(4,1)} %bitcast.37), calls=%async_computation.3 | async-start | bytes 8388608
  187.8 3.5 %slice-start.1 = ((s8[5898240]{0:T(1024)(128)(4,1)}), s8[1703936]{0:T(1024)(128)(4,1)S(1)}, s32[]{:S(2)}) async-start(s8[5898240]{0:T(1024)(128)(4,1)} %bitcast.37), calls=%async_computation.4 | async-start | bytes 3407872
Sparse Core Ops, SparseCore 0:
  37.5 45.6 all-gather.2
  206.7 77.7 reduce-scatter.1
